TPU v7x, 32 devices: a whole 2x2x4 slice. The times are simulated.
32 devices in a mesh: lat: 4 (over z), lon: 8 (over y, x, core).
Axes of the slice: x: 2, y: 2, z: 4, core: 2. Of those that a mesh axis runs over, the one named last changes fastest.
Arguments:
- latent: bfloat16 [48, 576, 512], P('lat', 'lon'), may hold values from -1000 to 1000
- w_qkv: bfloat16 [512, 1536], replicated, may hold values from -1 to 1
- w_proj: bfloat16 [512, 512], replicated, may hold values from -0.25 to 0.25
- w_fc1: bfloat16 [512, 2048], replicated, may hold values from -0.25 to 0.25
- w_fc2: bfloat16 [2048, 512], replicated, may hold values from -0.125 to 0.125
- w_head: bfloat16 [512, 1024], replicated, may hold values from -4 to 4
- target_bins: int32 [48, 576, 4], P('lat', 'lon'), may hold values from 0 to 255
- land_mask: int32 [48, 576], P('lat', 'lon'), may hold values 0 or 1
Outputs:
- grad_latent: bfloat16 [48, 576, 512], P('lat', 'lon')
- grad_qkv: float32 [512, 1536], P(('lat', 'lon'))
- grad_proj: float32 [512, 512], P(('lat', 'lon'))
- grad_fc1: float32 [512, 2048], P(('lat', 'lon'))
- grad_fc2: float32 [2048, 512], P(('lat', 'lon'))
- grad_head: float32 [512, 1024], P(('lat', 'lon'))
All inputs are finite; a program needn't handle non-finite values. No bound on the sum of `land_mask` on one device may be relied on, other than what follows from the above.
Results may differ from a plain program's by a relative error of at most 0.015.
Values may be sent and summed in bfloat16 or wider, within the bound.
A program may use at most 128 MiB of HBM per device.

v0:
```python
import math

import jax
import jax.numpy as jnp
from jax import lax
from jax.sharding import PartitionSpec as P

HEADS = 8
BINS = 256
VARS = 4
WIN_LAT = 6
WIN_LON = 12
HEAD_DIM = 64


eps = 1e-05
smear = 0.75
masked = -1e30


def shifted_2(value, axis, steps):
    count = lax.axis_size(axis)
    pairs = [(source, (source + steps) % count) for source in range(count)]
    return lax.ppermute(value, axis, pairs)


def normalize(values_in):
    centre = jnp.mean(values_in, -1, keepdims=True)
    offset = values_in - centre
    inverse = lax.rsqrt(jnp.mean(offset * offset, -1, keepdims=True) + eps)
    return (offset * inverse, inverse)


def norm_back(scaled, inverse, upstream):
    return inverse * (
        upstream
        - jnp.mean(upstream, -1, keepdims=True)
        - scaled * jnp.mean(upstream * scaled, -1, keepdims=True)
    )


def gelu_parts(pre_act):
    normal_cdf = 0.5 * (1.0 + jax.scipy.special.erf(pre_act / math.sqrt(2.0)))
    density = jnp.exp(-0.5 * pre_act * pre_act) / math.sqrt(2.0 * math.pi)
    return (pre_act * normal_cdf, normal_cdf + pre_act * density)


def mixing(form, left, right):
    return jnp.einsum(form, left, right, preferred_element_type=jnp.float32)


def to_windows(block):
    row_count, col_count, feat_count = block.shape
    shaped = block.reshape(row_count // WIN_LAT, WIN_LAT, col_count // WIN_LON, WIN_LON, feat_count)
    return shaped.transpose(0, 2, 1, 3, 4).reshape(-1, WIN_LAT * WIN_LON, feat_count)


def from_windows(packed, row_count, col_count):
    feat_count = packed.shape[-1]
    shaped = packed.reshape(
        row_count // WIN_LAT, col_count // WIN_LON, WIN_LAT, WIN_LON, feat_count
    )
    return shaped.transpose(0, 2, 1, 3, 4).reshape(row_count, col_count, feat_count)


def window_setup(qkv_all, row_labels):
    row_count, col_count, _ = qkv_all.shape
    packed = to_windows(qkv_all)
    heads_view = packed.reshape(packed.shape[0], packed.shape[1], 3, HEADS, HEAD_DIM)
    window_tags = to_windows(
        jnp.broadcast_to(row_labels[:, None, None], (row_count, col_count, 1))
    )[:, :, 0]
    allowed = window_tags[:, :, None] == window_tags[:, None, :]
    scores = mixing("wqhd,wkhd->whqk", heads_view[:, :, 0], heads_view[:, :, 1]) * HEAD_DIM ** (
        -0.5
    )
    scores = jnp.where(allowed[:, None], scores, masked)
    highest = jnp.max(scores, -1, keepdims=True)
    exponent = jnp.exp(scores - highest)
    return (heads_view, exponent / jnp.sum(exponent, -1, keepdims=True))


def window_forward(heads_view, attn_probs, row_count, col_count):
    context = mixing(
        "whqk,wkhd->wqhd", attn_probs.astype(jnp.bfloat16), heads_view[:, :, 2]
    ).astype(jnp.bfloat16)
    return from_windows(
        context.reshape(context.shape[0], context.shape[1], -1), row_count, col_count
    )


def window_backward(heads_view, attn_probs, d_context, row_count, col_count):
    probs_low = attn_probs.astype(jnp.bfloat16)
    upstream = to_windows(d_context).reshape(
        heads_view.shape[0], heads_view.shape[1], HEADS, HEAD_DIM
    )
    d_probs = mixing("wqhd,wkhd->whqk", upstream, heads_view[:, :, 2])
    d_value = mixing("whqk,wqhd->wkhd", probs_low, upstream)
    d_scores = (
        attn_probs
        * (d_probs - jnp.sum(d_probs * attn_probs, -1, keepdims=True))
        * HEAD_DIM ** (-0.5)
    )
    d_scores = d_scores.astype(jnp.bfloat16)
    d_query = mixing("whqk,wkhd->wqhd", d_scores, heads_view[:, :, 1])
    d_key = mixing("whqk,wqhd->wkhd", d_scores, heads_view[:, :, 0])
    joined = jnp.stack([d_query, d_key, d_value], 2).astype(jnp.bfloat16)
    return from_windows(joined.reshape(joined.shape[0], joined.shape[1], -1), row_count, col_count)


def hl_target(bin_index):
    bin_edges = jnp.arange(BINS + 1, dtype=jnp.int32).astype(jnp.float32)
    centre = bin_index.astype(jnp.float32)[..., None] + 0.5
    cumulative = 0.5 * jax.scipy.special.erf((bin_edges - centre) / (smear * math.sqrt(2.0)))
    return (cumulative[..., 1:] - cumulative[..., :-1]) / (
        cumulative[..., -1:] - cumulative[..., :1]
    )


def head_grad(normed3, w_head, target_bins, land_mask):
    logits = jnp.dot(normed3, w_head, preferred_element_type=jnp.float32).reshape(-1, VARS, BINS)
    highest = jnp.max(logits, -1, keepdims=True)
    exponent = jnp.exp(logits - highest)
    bin_probs = exponent / jnp.sum(exponent, -1, keepdims=True)
    weight_tok = land_mask.reshape(-1).astype(jnp.float32)[:, None, None] / VARS
    d_logits = weight_tok * (bin_probs - hl_target(target_bins.reshape(-1, VARS)))
    return d_logits.astype(jnp.bfloat16).reshape(-1, VARS * BINS)


def roll_ahead(block):
    half_rows = WIN_LAT // 2
    half_cols = WIN_LON // 2
    edge_cols = shifted_2(block[:, :half_cols], "lon", -1)
    moved_cols = jnp.concatenate([block[:, half_cols:], edge_cols], 1)
    edge_rows = shifted_2(moved_cols[:half_rows], "lat", -1)
    return jnp.concatenate([moved_cols[half_rows:], edge_rows], 0)


def roll_behind(block):
    half_rows = WIN_LAT // 2
    half_cols = WIN_LON // 2
    row_count, col_count = (block.shape[0], block.shape[1])
    edge_cols = shifted_2(block[:, col_count - half_cols :], "lon", 1)
    moved_cols = jnp.concatenate([edge_cols, block[:, : col_count - half_cols]], 1)
    edge_rows = shifted_2(moved_cols[row_count - half_rows :], "lat", 1)
    return jnp.concatenate([edge_rows, moved_cols[: row_count - half_rows]], 0)


def local(latent, w_qkv, w_proj, w_fc1, w_fc2, w_head, target_bins, land_mask):
    row_count, col_count, feat_width = latent.shape
    half_rows = WIN_LAT // 2
    lat_total = row_count * lax.axis_size("lat")
    row_place = (
        lax.axis_index("lat") * row_count + jnp.arange(row_count, dtype=jnp.int32) + half_rows
    )
    row_labels = (row_place >= lat_total).astype(jnp.int32)
    residual_in = latent.astype(jnp.float32)
    scaled1, inverse1 = normalize(residual_in)
    normed1 = scaled1.astype(jnp.bfloat16)
    shifted = roll_ahead(normed1)
    shifted_flat = shifted.reshape(-1, feat_width)
    qkv_all = jnp.dot(shifted_flat, w_qkv, preferred_element_type=jnp.float32).astype(jnp.bfloat16)
    qkv_all = qkv_all.reshape(row_count, col_count, 3 * feat_width)
    heads_view, attn_probs = window_setup(qkv_all, row_labels)
    context = window_forward(heads_view, attn_probs, row_count, col_count).reshape(-1, feat_width)
    attended = jnp.dot(context, w_proj, preferred_element_type=jnp.float32).astype(jnp.bfloat16)
    attended = attended.reshape(row_count, col_count, feat_width)
    attended = roll_behind(attended)
    residual = residual_in + attended.astype(jnp.float32)
    scaled2, inverse2 = normalize(residual)
    normed2 = scaled2.astype(jnp.bfloat16).reshape(-1, feat_width)
    pre_act = jnp.dot(normed2, w_fc1, preferred_element_type=jnp.float32)
    activated, gelu_slope = gelu_parts(pre_act)
    activated = activated.astype(jnp.bfloat16)
    block_out = residual + jnp.dot(activated, w_fc2, preferred_element_type=jnp.float32).reshape(
        row_count, col_count, feat_width
    )
    scaled3, inverse3 = normalize(block_out)
    normed3 = scaled3.astype(jnp.bfloat16).reshape(-1, feat_width)
    d_logits = head_grad(normed3, w_head, target_bins, land_mask)
    grad_head = jnp.dot(normed3.T, d_logits, preferred_element_type=jnp.float32)
    d_out = norm_back(
        scaled3,
        inverse3,
        jnp.dot(d_logits, w_head.T, preferred_element_type=jnp.float32).reshape(
            row_count, col_count, feat_width
        ),
    )
    d_outb = d_out.astype(jnp.bfloat16).reshape(-1, feat_width)
    grad_fc2 = jnp.dot(activated.T, d_outb, preferred_element_type=jnp.float32)
    d_pre = (jnp.dot(d_outb, w_fc2.T, preferred_element_type=jnp.float32) * gelu_slope).astype(
        jnp.bfloat16
    )
    grad_fc1 = jnp.dot(normed2.T, d_pre, preferred_element_type=jnp.float32)
    d_resid = d_out + norm_back(
        scaled2,
        inverse2,
        jnp.dot(d_pre, w_fc1.T, preferred_element_type=jnp.float32).reshape(
            row_count, col_count, feat_width
        ),
    )
    d_attended = d_resid.astype(jnp.bfloat16)
    d_attended = roll_ahead(d_attended)
    d_attended = d_attended.reshape(-1, feat_width)
    grad_proj = jnp.dot(context.T, d_attended, preferred_element_type=jnp.float32)
    d_context = jnp.dot(d_attended, w_proj.T, preferred_element_type=jnp.float32).astype(
        jnp.bfloat16
    )
    d_context = d_context.reshape(row_count, col_count, feat_width)
    d_qkv = window_backward(heads_view, attn_probs, d_context, row_count, col_count).reshape(
        -1, 3 * feat_width
    )
    grad_qkv = jnp.dot(shifted_flat.T, d_qkv, preferred_element_type=jnp.float32)
    d_shifted = jnp.dot(d_qkv, w_qkv.T, preferred_element_type=jnp.float32).astype(jnp.bfloat16)
    d_shifted = d_shifted.reshape(row_count, col_count, feat_width)
    d_shifted = roll_behind(d_shifted)
    grad_latent = (d_resid + norm_back(scaled1, inverse1, d_shifted.astype(jnp.float32))).astype(
        jnp.bfloat16
    )
    lat_reduced = (
        lax.psum_scatter(
            grad_qkv.astype(jnp.bfloat16), "lat", scatter_dimension=0, tiled=True
        ).astype(jnp.float32),
        lax.psum_scatter(
            grad_proj.astype(jnp.bfloat16), "lat", scatter_dimension=0, tiled=True
        ).astype(jnp.float32),
        lax.psum_scatter(
            grad_fc1.astype(jnp.bfloat16), "lat", scatter_dimension=0, tiled=True
        ).astype(jnp.float32),
        lax.psum_scatter(
            grad_fc2.astype(jnp.bfloat16), "lat", scatter_dimension=0, tiled=True
        ).astype(jnp.float32),
        lax.psum_scatter(
            grad_head.astype(jnp.bfloat16), "lat", scatter_dimension=0, tiled=True
        ).astype(jnp.float32),
    )
    summed = (
        lax.psum_scatter(
            lat_reduced[0].astype(jnp.bfloat16), "lon", scatter_dimension=0, tiled=True
        ).astype(jnp.float32),
        lax.psum_scatter(
            lat_reduced[1].astype(jnp.bfloat16), "lon", scatter_dimension=0, tiled=True
        ).astype(jnp.float32),
        lax.psum_scatter(
            lat_reduced[2].astype(jnp.bfloat16), "lon", scatter_dimension=0, tiled=True
        ).astype(jnp.float32),
        lax.psum_scatter(
            lat_reduced[3].astype(jnp.bfloat16), "lon", scatter_dimension=0, tiled=True
        ).astype(jnp.float32),
        lax.psum_scatter(
            lat_reduced[4].astype(jnp.bfloat16), "lon", scatter_dimension=0, tiled=True
        ).astype(jnp.float32),
    )
    return (grad_latent, summed[0], summed[1], summed[2], summed[3], summed[4])


def solution(mesh):
    placed = (
        P("lat", "lon", None),
        P(),
        P(),
        P(),
        P(),
        P(),
        P("lat", "lon", None),
        P("lat", "lon"),
    )
    return jax.shard_map(
        local,
        mesh=mesh,
        in_specs=placed,
        out_specs=(
            P("lat", "lon", None),
            P(("lat", "lon"), None),
            P(("lat", "lon"), None),
            P(("lat", "lon"), None),
            P(("lat", "lon"), None),
            P(("lat", "lon"), None),
        ),
        check_vma=False,
    )
```

profile of v0, /device:TPU:0, one launch (start us, length us, event | category | flops | bytes accessed | tf_op | source)
XLA Modules:
  0.0 569.0 jit_solution(11099422243711899693)
XLA Ops:
  11.8 3.4 collective-permute-start
  15.6 2.3 slice.95
  19.1 3.7 collective-permute-start.1
  22.8 3.9 collective-permute-done.1
  27.7 3.1 convolution_convert_fusion
  30.8 5.1 reshape_reshape.22
  35.9 4.1 copy.20
  40.1 8.1 %reshape_reshape.23 = bf16[12,72,3,8,64]{4,3,2,1,0:T(8,128)(2,1)} reshape(bf16[2,6,6,12,1536]{4,3,2,1,0:T(8,128)(2,1)} %copy.20) | data formatting | bytes 5308416 | tf_op jit(solution)/shard_map/reshape;reshape | solution.py:69
  48.2 5.1 fusion.96
  53.2 3.8 copy.45
  57.0 3.8 copy.44
  60.9 3.8 copy.46
  64.7 3.1 fusion.47
  72.9 3.8 copy.25
  76.7 3.8 reshape_reshape.24
  80.5 2.4 copy.26
  83.0 2.1 reshape_reshape.25
  85.1 1.9 convolution_convert_fusion.9
  87.1 3.0 erf_multiply_fusion
  90.2 1.9 collective-permute-done.2
  93.5 2.3 copy.43
  95.8 2.7 fusion.34
  98.4 2.5 collective-permute-done.3
  102.8 4.6 multiply_convert_fusion
  107.4 2.0 fusion.99
  111.7 4.7 fusion.1
  116.4 12.0 %fusion.14 = bf16[864,4,256]{2,0,1:T(8,128)(2,1)} fusion(f32[864,4,257]{2,0,1:T(8,128)} %erf_multiply_fusion, f32[864,4,256]{2,0,1:T(8,128)} %fusion.1, f32[864,4]{0,1:T(4,128)S(1)} %fusion.34, f32[864]{0:T(1024)S(1)} %copy-done.30, bf16[864,512,1]{1,0,2:T(8,128)(2,1)} %bitcast.123, bf16[4,256,512]{2,1,0:T(8,128)(2,1)} %bitcast.118), kind=kOutput, calls=%fused_computation.25 | convolution fusion | flops 912166528 | bytes 14336896 | tf_op jit(solution)/shard_map/sub | solution.py:123
  128.4 4.1 copy.29
  132.5 4.2 dot_general.78
  136.7 3.9 fusion.92
  143.0 6.5 %fusion.9 = bf16[864,2048]{1,0:T(8,128)(2,1)S(1)} fusion(f32[864,2048]{1,0:T(8,128)} %get-tuple-element.20, bf16[864,512]{1,0:T(8,128)(2,1)S(1)} %bitcast.131, bf16[2048,512]{1,0:T(8,128)(2,1)S(1)} %copy-done.32), kind=kOutput, calls=%fused_computation.10 | convolution fusion | flops 1829634048 | bytes 13598720 | tf_op jit(solution)/shard_map/dot_general | solution.py:191
  149.5 3.3 fusion.98
  152.9 2.6 multiply_reduce_fusion.1
  155.6 4.7 fusion.93
  160.3 2.0 collective-permute-start.4
  162.5 2.0 collective-permute-done.4
  166.1 4.8 collective-permute-done.5
  173.5 2.4 copy.38
  175.9 4.2 convolution_convert_fusion.6
  182.2 3.1 reshape_reshape.27
  185.3 2.3 copy.31
  187.6 5.0 fusion.51
  192.6 7.7 %fusion.63 = bf16[12,72,1,8,64]{1,4,3,0,2:T(8,128)(2,1)} fusion(f32[12,8,72,72]{2,3,1,0:T(8,128)} %fusion.51, bf16[12,72,1,8,64]{1,4,3,0,2:T(8,128)(2,1)S(1)} %copy-done.13, f32[12,8,72,72]{2,3,1,0:T(8,128)} %copy-done.37, f32[12,8,72]{2,1,0:T(8,128)S(1)} %copy-done.39), kind=kOutput, calls=%fused_computation.80 | convolution fusion | flops 67633992 | bytes 5778432 | tf_op jit(solution)/shard_map/whqk,wqhd->wkhd/dot_general | solution.py:49
  200.3 8.3 %fusion.54 = bf16[12,72,1,8,64]{1,4,3,0,2:T(8,128)(2,1)} fusion(f32[12,8,72,72]{2,3,1,0:T(8,128)} %fusion.51, bf16[12,72,1,8,64]{1,4,3,0,2:T(8,128)(2,1)} %copy.46, f32[12,8,72,72]{2,3,1,0:T(8,128)} %copy-done.37, f32[12,8,72]{2,1,0:T(8,128)S(1)} %copy-done.39), kind=kOutput, calls=%fused_computation.77 | convolution fusion | flops 67633992 | bytes 5778432 | tf_op jit(solution)/shard_map/whqk,wkhd->wqhd/dot_general | solution.py:49
  208.6 3.2 fusion.62
  211.9 2.8 pad_maximum_fusion
  214.7 8.7 %copy.36 = bf16[12,72,3,8,64]{4,3,2,1,0:T(8,128)(2,1)} copy(bf16[12,72,3,8,64]{1,4,3,0,2:T(8,128)(2,1)} %pad_maximum_fusion) | data formatting | bytes 5308416 | tf_op jit(solution)/shard_map/stack | solution.py:107
  223.4 8.2 %convert_element_type.157 = bf16[2,6,6,12,1536]{4,3,2,1,0:T(8,128)(2,1)} reshape(bf16[12,72,3,8,64]{4,3,2,1,0:T(8,128)(2,1)} %copy.36) | data formatting | bytes 5308416 | tf_op jit(solution)/shard_map/convert_element_type | solution.py:107
  231.6 4.1 copy.37
  235.7 5.3 reshape_reshape.28
  241.1 4.8 convolution_convert_fusion.3
  245.9 5.7 %convolution_convert_fusion.1 = bf16[2048,512]{1,0:T(8,128)(2,1)} fusion(bf16[864,2048]{1,0:T(8,128)(2,1)} %copy-done.36, bf16[864,512]{1,0:T(8,128)(2,1)S(1)} %bitcast.132), kind=kOutput, calls=%fused_computation.27 | convolution fusion | flops 1812987904 | bytes 6520832 | tf_op jit(solution)/shard_map/dot_general | solution.py:190
  252.8 5.8 %convolution_convert_fusion.2 = bf16[512,2048]{1,0:T(8,128)(2,1)} fusion(bf16[864,512]{1,0:T(8,128)(2,1)S(1)} %bitcast.128, bf16[864,2048]{1,0:T(8,128)(2,1)} %copy-done.35), kind=kOutput, calls=%fused_computation.28 | convolution fusion | flops 1812987904 | bytes 6520832 | tf_op jit(solution)/shard_map/dot_general | solution.py:194
  260.1 22.3 %reduce-scatter.11.cloned.1.call-done = bf16[128,1536]{1,0:T(8,128)(2,1)} async-done(((bf16[512,1536]{1,0:T(8,128)(2,1)}), bf16[128,1536]{1,0:T(8,128)(2,1)}) %reduce-scatter.11.cloned.1.call-update) | async-done | bytes 393232 | tf_op jit(solution)/shard_map/reduce_scatter | solution.py:221
  282.5 44.6 %reduce-scatter.23.cloned.1.call-done = bf16[512,512]{1,0:T(8,128)(2,1)} async-done(((bf16[2048,512]{1,0:T(8,128)(2,1)}), bf16[512,512]{1,0:T(8,128)(2,1)}) %reduce-scatter.23.cloned.1.call-update) | async-done | bytes 524304 | tf_op jit(solution)/shard_map/reduce_scatter | solution.py:230
  327.1 3.8 convolution_convert_fusion.7
  331.0 4.9 collective-permute-done.6
  336.7 40.1 %reduce-scatter.19.cloned.1.call-done = bf16[128,2048]{1,0:T(8,128)(2,1)} async-done(((bf16[512,2048]{1,0:T(8,128)(2,1)}), bf16[128,2048]{1,0:T(8,128)(2,1)}) %reduce-scatter.19.cloned.1.call-update) | async-done | bytes 524304 | tf_op jit(solution)/shard_map/reduce_scatter | solution.py:227
  378.1 3.1 fusion.31
  381.2 31.4 %reduce-scatter.17.cloned.1.call-done = bf16[16,512]{1,0:T(8,128)(2,1)} async-done(((bf16[128,512]{1,0:T(8,128)(2,1)}), bf16[16,512]{1,0:T(8,128)(2,1)}) %reduce-scatter.17.cloned.1.call-update) | async-done | bytes 16400 | tf_op jit(solution)/shard_map/reduce_scatter | solution.py:241
  413.9 35.4 %reduce-scatter.29.cloned.1.call-done = bf16[16,1024]{1,0:T(8,128)(2,1)} async-done(((bf16[128,1024]{1,0:T(8,128)(2,1)}), bf16[16,1024]{1,0:T(8,128)(2,1)}) %reduce-scatter.29.cloned.1.call-update) | async-done | bytes 32784 | tf_op jit(solution)/shard_map/reduce_scatter | solution.py:250
  450.6 35.6 %reduce-scatter.13.cloned.1.call-done = bf16[16,1536]{1,0:T(8,128)(2,1)} async-done(((bf16[128,1536]{1,0:T(8,128)(2,1)}), bf16[16,1536]{1,0:T(8,128)(2,1)}) %reduce-scatter.13.cloned.1.call-update) | async-done | bytes 49168 | tf_op jit(solution)/shard_map/reduce_scatter | solution.py:238
  487.7 35.8 %reduce-scatter.25.cloned.1.call-done = bf16[64,512]{1,0:T(8,128)(2,1)} async-done(((bf16[512,512]{1,0:T(8,128)(2,1)}), bf16[64,512]{1,0:T(8,128)(2,1)}) %reduce-scatter.25.cloned.1.call-update) | async-done | bytes 65552 | tf_op jit(solution)/shard_map/reduce_scatter | solution.py:247
  525.0 35.6 %reduce-scatter.21.cloned.1.call-done = bf16[16,2048]{1,0:T(8,128)(2,1)} async-done(((bf16[128,2048]{1,0:T(8,128)(2,1)}), bf16[16,2048]{1,0:T(8,128)(2,1)}) %reduce-scatter.21.cloned.1.call-update) | async-done | bytes 65552 | tf_op jit(solution)/shard_map/reduce_scatter | solution.py:244
  (166 shorter events, 38.6 us)
Async XLA Ops:
  7.2 95.6 %copy-start = (bf16[512,2048]{1,0:T(8,128)(2,1)S(1)}, bf16[512,2048]{1,0:T(8,128)(2,1)}, u32[]{:S(2)}) copy-start(bf16[512,2048]{1,0:T(8,128)(2,1)} %param.11) | copy-start | bytes 6291460
  7.2 3.4 copy-start.2
  7.2 251.6 %reduce-scatter.15.cloned.1.call-start = ((), (), s32[]{:S(2)}) async-start(), calls=%async_computation.12 | async-start | bytes 655360 | tf_op jit(solution)/shard_map/reduce_scatter | solution.py:224
  8.9 6.7 %copy-start.28 = (s32[12,72,4]{1,2,0:T(4,128)S(1)}, s32[12,72,4]{1,2,0:T(4,128)}, u32[]{:S(2)}) copy-start(s32[12,72,4]{1,2,0:T(4,128)} %param.14) | copy-start | bytes 41476
  10.9 0.9 copy-start.16
  11.8 6.2 %collective-permute-start = (bf16[12,6,512]{2,1,0:T(8,128)(2,1)S(1)}, bf16[12,6,512]{2,1,0:T(8,128)(2,1)S(1)}, u32[]{:S(2)}, u32[]{:S(2)}) collective-permute-start(bf16[12,6,512]{2,1,0:T(8,128)(2,1)S(1)} %slice.96), channel_id=1, source_target_pairs={{0,7},{1,0},{2,1},{3,2},{4,3},{5,4},{6,5},{7,6},{8,15},{9,8},{10,9... | collective-permute-start | bytes 221192 | tf_op jit(solution)/shard_map/ppermute | solution.py:24
  18.0 4.7 copy-start.10
  19.0 8.7 %copy-start.33 = (bf16[512,1536]{1,0:T(8,128)(2,1)S(1)}, bf16[512,1536]{1,0:T(8,128)(2,1)}, u32[]{:S(2)}) copy-start(bf16[512,1536]{1,0:T(8,128)(2,1)} %param.9) | copy-start | bytes 4718596
  19.1 7.6 %collective-permute-start.1 = (bf16[3,72,512]{2,1,0:T(8,128)(2,1)S(1)}, bf16[3,72,512]{2,1,0:T(8,128)(2,1)S(1)}, u32[]{:S(2)}, u32[]{:S(2)}) collective-permute-start(bf16[3,72,512]{2,1,0:T(8,128)(2,1)S(1)} %pad_maximum_fusion.8), channel_id=1, source_target_pairs={{0,24},{8,0},{16,8},{24,16},{1,25},{9,1},{17,9},{25,17},{2,26},{10... | collective-permute-start | bytes 663560 | tf_op jit(solution)/shard_map/ppermute | solution.py:24
  26.8 0.9 copy-start.19
  67.8 3.2 copy-start.14
  69.2 1.8 copy-start.37
  69.2 3.7 copy-start.38
  87.0 5.1 copy-start.3
  87.0 5.8 %copy-start.29 = (s32[12,72]{1,0:T(8,128)S(1)}, s32[12,72]{1,0:T(8,128)}, u32[]{:S(2)}) copy-start(s32[12,72]{1,0:T(8,128)} %param.15) | copy-start | bytes 10372
  87.0 5.0 collective-permute-start.2
  92.1 8.9 %collective-permute-start.3 = (bf16[3,72,512]{2,1,0:T(8,128)(2,1)S(1)}, bf16[3,72,512]{2,1,0:T(8,128)(2,1)S(1)}, u32[]{:S(2)}, u32[]{:S(2)}) collective-permute-start(bf16[3,72,512]{2,1,0:T(8,128)(2,1)S(1)} %pad_maximum_fusion.7), channel_id=1, source_target_pairs={{0,8},{8,16},{16,24},{24,0},{1,9},{9,17},{17,25},{25,1},{2,10},{10... | collective-permute-start | bytes 663560 | tf_op jit(solution)/shard_map/ppermute | solution.py:24
  95.8 5.2 copy-start.4
  102.7 4.7 copy-start.21
  102.8 4.7 copy-start.31
  107.4 2.0 copy-start.36
  109.9 1.7 copy-start.6
  111.7 4.7 copy-start.30
  136.7 3.9 copy-start.7
  140.6 1.2 copy-start.12
  140.6 2.4 copy-start.32
  141.8 7.7 %copy-start.26 = (bf16[12,72,512]{2,1,0:T(8,128)(2,1)}, bf16[12,72,512]{2,1,0:T(8,128)(2,1)S(1)}, u32[]{:S(2)}) copy-start(bf16[12,72,512]{2,1,0:T(8,128)(2,1)S(1)} %fusion.80) | copy-start | bytes 2654212
  149.5 3.3 copy-start.35
  152.9 2.7 copy-start.5
  152.9 2.7 copy-start.8
  160.3 4.2 collective-permute-start.4
  164.5 7.4 %copy-start.25 = (bf16[864,512]{1,0:T(8,128)(2,1)S(1)}, bf16[864,512]{1,0:T(8,128)(2,1)}, u32[]{:S(2)}) copy-start(bf16[864,512]{1,0:T(8,128)(2,1)} %reshape_reshape.25) | copy-start | bytes 2654212
  164.5 6.4 %collective-permute-start.5 = (bf16[3,72,512]{2,1,0:T(8,128)(2,1)S(1)}, bf16[3,72,512]{2,1,0:T(8,128)(2,1)S(1)}, u32[]{:S(2)}, u32[]{:S(2)}) collective-permute-start(bf16[3,72,512]{2,1,0:T(8,128)(2,1)S(1)} %pad_maximum_fusion.6), channel_id=1, source_target_pairs={{0,24},{8,0},{16,8},{24,16},{1,25},{9,1},{17,9},{25,17},{2,26},{10... | collective-permute-start | bytes 663560 | tf_op jit(solution)/shard_map/ppermute | solution.py:24
  171.0 0.9 copy-start.23
  171.9 1.6 copy-start.11
  173.5 85.9 %reduce-scatter.27.cloned.1.call-start = ((), (), s32[]{:S(2)}) async-start(), calls=%async_computation.18 | async-start | bytes 1310720 | tf_op jit(solution)/shard_map/reduce_scatter | solution.py:233
  175.9 4.3 copy-start.24
  175.9 4.3 copy-start.34
  180.1 102.3 %reduce-scatter.11.cloned.1.call-start = ((), (), s32[]{:S(2)}) async-start(), calls=%async_computation.10 | async-start | bytes 1966080 | tf_op jit(solution)/shard_map/reduce_scatter | solution.py:221
  187.6 5.0 copy-start.13
  187.6 5.0 copy-start.39
  200.3 8.3 %copy-start.15 = (bf16[12,72,8,64]{1,3,2,0:T(8,128)(2,1)S(1)}, bf16[12,72,8,64]{1,3,2,0:T(8,128)(2,1)}, u32[]{:S(2)}) copy-start(bf16[12,72,8,64]{1,3,2,0:T(8,128)(2,1)} %copy.31) | copy-start | bytes 2654212
  208.6 3.2 copy-start.17
  208.6 3.2 copy-start.18
  235.7 5.3 copy-start.20
  241.1 4.9 copy-start.27
  245.9 81.2 %reduce-scatter.23.cloned.1.call-start = ((), (), s32[]{:S(2)}) async-start(), calls=%async_computation.16 | async-start | bytes 2621440 | tf_op jit(solution)/shard_map/reduce_scatter | solution.py:230
  251.7 1.2 copy-start.22
  251.7 125.1 %reduce-scatter.19.cloned.1.call-start = ((), (), s32[]{:S(2)}) async-start(), calls=%async_computation.14 | async-start | bytes 2621440 | tf_op jit(solution)/shard_map/reduce_scatter | solution.py:227
  258.7 153.8 %reduce-scatter.17.cloned.1.call-start = ((), (), s32[]{:S(2)}) async-start(), calls=%async_computation.13 | async-start | bytes 147456 | tf_op jit(solution)/shard_map/reduce_scatter | solution.py:241
  259.3 190.0 %reduce-scatter.29.cloned.1.call-start = ((), (), s32[]{:S(2)}) async-start(), calls=%async_computation.19 | async-start | bytes 294912 | tf_op jit(solution)/shard_map/reduce_scatter | solution.py:250
  260.0 226.2 %reduce-scatter.13.cloned.1.call-start = ((), (), s32[]{:S(2)}) async-start(), calls=%async_computation.11 | async-start | bytes 442368 | tf_op jit(solution)/shard_map/reduce_scatter | solution.py:238
  282.4 241.0 %reduce-scatter.25.cloned.1.call-start = ((), (), s32[]{:S(2)}) async-start(), calls=%async_computation.17 | async-start | bytes 589824 | tf_op jit(solution)/shard_map/reduce_scatter | solution.py:247
  327.1 233.4 %reduce-scatter.21.cloned.1.call-start = ((), (), s32[]{:S(2)}) async-start(), calls=%async_computation.15 | async-start | bytes 589824 | tf_op jit(solution)/shard_map/reduce_scatter | solution.py:244
  330.9 47.1 %copy-start.9 = (bf16[864,512]{1,0:T(8,128)(2,1)}, bf16[864,512]{1,0:T(8,128)(2,1)S(1)}, u32[]{:S(2)}) copy-start(bf16[864,512]{1,0:T(8,128)(2,1)S(1)} %convolution_convert_fusion.7) | copy-start | bytes 2654212
  331.0 5.0 collective-permute-start.6
  336.0 40.8 %collective-permute-start.7 = (bf16[3,72,512]{2,1,0:T(8,128)(2,1)S(1)}, bf16[3,72,512]{2,1,0:T(8,128)(2,1)S(1)}, u32[]{:S(2)}, u32[]{:S(2)}) collective-permute-start(bf16[3,72,512]{2,1,0:T(8,128)(2,1)S(1)} %pad_maximum_fusion.5), channel_id=1, source_target_pairs={{0,8},{8,16},{16,24},{24,0},{1,9},{9,17},{17,25},{25,1},{2,10},{10... | collective-permute-start | bytes 663560 | tf_op jit(solution)/shard_map/ppermute | solution.py:24
  378.0 184.0 %copy-start.1 = (bf16[512,2048]{1,0:T(8,128)(2,1)S(1)}, bf16[512,2048]{1,0:T(8,128)(2,1)}, u32[]{:S(2)}) copy-start(bf16[512,2048]{1,0:T(8,128)(2,1)} %param.11) | copy-start | bytes 6291460
Sparse Core Ops, SparseCore 0:
  173.6 22.7 reduce-scatter.14
  198.7 25.5 reduce-scatter.26
  246.0 36.3 reduce-scatter.10
  284.5 42.4 reduce-scatter.22
  329.2 47.5 reduce-scatter.18
  379.7 32.8 reduce-scatter.16
  415.5 33.6 reduce-scatter.28
  452.3 33.8 reduce-scatter.12
  489.3 34.0 reduce-scatter.24
  526.4 34.0 reduce-scatter.20
where the time goes:
time: 578 us; the launch traced here: 569 us
  waiting for transfers between devices  302 us (52%)
  local copies, waits for them, and re-layouts  103 us (18%)
  matrix products  97.6 us (17%)
  other arithmetic  38.4 us (7%)
  between operations  15.1 us (3%)
  starting transfers between devices  12.7 us (2%)
    reduce_scatter x1, waiting for transfers between devices, local(): lax.psum_scatter(grad_fc2.astype(jnp.bfloat16), 'lat', scatter_dimension=...  44.6 us
    reduce_scatter x1, waiting for transfers between devices, local(): lax.psum_scatter(grad_fc1.astype(jnp.bfloat16), 'lat', scatter_dimension=...  40.1 us
    reduce_scatter x1, waiting for transfers between devices, local(): lax.psum_scatter(lat_reduced[3].astype(jnp.bfloat16), 'lon', scatter_dime...  35.8 us
    reduce_scatter x1, waiting for transfers between devices, local(): lax.psum_scatter(lat_reduced[0].astype(jnp.bfloat16), 'lon', scatter_dime...  35.6 us
    reduce_scatter x1, waiting for transfers between devices, local(): lax.psum_scatter(lat_reduced[2].astype(jnp.bfloat16), 'lon', scatter_dime...  35.6 us
    reduce_scatter x1, waiting for transfers between devices, local(): lax.psum_scatter(lat_reduced[4].astype(jnp.bfloat16), 'lon', scatter_dime...  35.4 us
    reduce_scatter x1, waiting for transfers between devices, local(): lax.psum_scatter(lat_reduced[1].astype(jnp.bfloat16), 'lon', scatter_dime...  31.4 us
    dot_general x6, matrix products, mixing(): return jnp.einsum(form, left, right, preferred_element_type=jnp.float32)  29.1 us
  transfers between devices with their start and end apart: 18, of which 14 were waited for; matrix products, arithmetic and copies ran while one was open for 19% of the time, Pallas kernels for 0%

commit v1 on v0

v1 whole, which is shorter than its diff:
```python
import math

import jax
import jax.numpy as jnp
from jax import lax
from jax.experimental import pallas as pl
from jax.experimental.pallas import tpu as pltpu
from jax.sharding import PartitionSpec as P

HEADS = 8
BINS = 256
VARS = 4
WIN_LAT = 6
WIN_LON = 12
HEAD_DIM = 64


eps = 1e-05
smear = 0.75
masked = -1e30


def shifted_2(value, axis, steps):
    count = lax.axis_size(axis)
    pairs = [(source, (source + steps) % count) for source in range(count)]
    return lax.ppermute(value, axis, pairs)


def normalize(values_in):
    centre = jnp.mean(values_in, -1, keepdims=True)
    offset = values_in - centre
    inverse = lax.rsqrt(jnp.mean(offset * offset, -1, keepdims=True) + eps)
    return (offset * inverse, inverse)


def norm_back(scaled, inverse, upstream):
    return inverse * (
        upstream
        - jnp.mean(upstream, -1, keepdims=True)
        - scaled * jnp.mean(upstream * scaled, -1, keepdims=True)
    )


def gelu_parts(pre_act):
    normal_cdf = 0.5 * (1.0 + jax.scipy.special.erf(pre_act / math.sqrt(2.0)))
    density = jnp.exp(-0.5 * pre_act * pre_act) / math.sqrt(2.0 * math.pi)
    return (pre_act * normal_cdf, normal_cdf + pre_act * density)


def dot_over(left, right, left_dim, right_dim):
    return lax.dot_general(
        left, right, (((left_dim,), (right_dim,)), ((), ())), preferred_element_type=jnp.float32
    )


def to_windows(block):
    row_count, col_count, feat_count = block.shape
    shaped = block.reshape(row_count // WIN_LAT, WIN_LAT, col_count // WIN_LON, WIN_LON, feat_count)
    return shaped.transpose(0, 2, 1, 3, 4).reshape(-1, feat_count)


def from_windows(packed, row_count, col_count):
    feat_count = packed.shape[-1]
    shaped = packed.reshape(
        row_count // WIN_LAT, col_count // WIN_LON, WIN_LAT, WIN_LON, feat_count
    )
    return shaped.transpose(0, 2, 1, 3, 4).reshape(row_count, col_count, feat_count)


def head_part(ref, part, head, width):
    start = part * width + head * HEAD_DIM
    return ref[0, :, start : start + HEAD_DIM]


def attention_kernel(qkv_ref, allowed_ref, context_ref, probs_ref):
    width = context_ref.shape[-1]
    allowed = allowed_ref[0] > 0.5
    pieces = []
    for head in range(HEADS):
        query = head_part(qkv_ref, 0, head, width)
        key = head_part(qkv_ref, 1, head, width)
        value = head_part(qkv_ref, 2, head, width)
        scores = dot_over(query, key, 1, 1) * HEAD_DIM ** (-0.5)
        scores = jnp.where(allowed, scores, masked)
        exponent = jnp.exp(scores - jnp.max(scores, -1, keepdims=True))
        probs = exponent / jnp.sum(exponent, -1, keepdims=True)
        probs_ref[0, head] = probs
        pieces.append(dot_over(probs.astype(jnp.bfloat16), value, 1, 0))
    context_ref[0] = jnp.concatenate(pieces, -1).astype(jnp.bfloat16)


def attention_back_kernel(qkv_ref, probs_ref, d_context_ref, d_qkv_ref):
    width = d_context_ref.shape[-1]
    d_queries, d_keys, d_values = [], [], []
    for head in range(HEADS):
        query = head_part(qkv_ref, 0, head, width)
        key = head_part(qkv_ref, 1, head, width)
        value = head_part(qkv_ref, 2, head, width)
        upstream = head_part(d_context_ref, 0, head, width)
        probs = probs_ref[0, head]
        d_probs = dot_over(upstream, value, 1, 1)
        d_scores = (
            probs
            * (d_probs - jnp.sum(d_probs * probs, -1, keepdims=True))
            * HEAD_DIM ** (-0.5)
        )
        d_scores_t = d_scores.T.astype(jnp.bfloat16)
        d_scores = d_scores.astype(jnp.bfloat16)
        d_queries.append(dot_over(d_scores, key, 1, 0))
        d_keys.append(dot_over(d_scores_t, query, 1, 0))
        d_values.append(dot_over(probs.T.astype(jnp.bfloat16), upstream, 1, 0))
    for part, pieces in enumerate((d_queries, d_keys, d_values)):
        joined = jnp.concatenate(pieces, -1).astype(jnp.bfloat16)
        d_qkv_ref[0, :, part * width : (part + 1) * width] = joined


def whole_block(*dims):
    return pl.BlockSpec((1, *dims), lambda place: (place,) + (0,) * len(dims))


def attention(qkv_all, allowed, windows_across):
    windows, tokens, triple = qkv_all.shape
    width = triple // 3
    return pl.pallas_call(
        attention_kernel,
        grid=(windows,),
        in_specs=[
            whole_block(tokens, triple),
            pl.BlockSpec((1, tokens, tokens), lambda place: (place // windows_across, 0, 0)),
        ],
        out_specs=[whole_block(tokens, width), whole_block(HEADS, tokens, tokens)],
        out_shape=[
            jax.ShapeDtypeStruct((windows, tokens, width), jnp.bfloat16),
            jax.ShapeDtypeStruct((windows, HEADS, tokens, tokens), jnp.float32),
        ],
        cost_estimate=pl.CostEstimate(
            flops=4 * windows * tokens * tokens * width * 20, bytes_accessed=8000000, transcendentals=0
        ),
        name="attention",
    )(qkv_all, allowed)


def attention_back(qkv_all, probs, d_context):
    windows, tokens, triple = qkv_all.shape
    width = triple // 3
    return pl.pallas_call(
        attention_back_kernel,
        grid=(windows,),
        in_specs=[
            whole_block(tokens, triple),
            whole_block(HEADS, tokens, tokens),
            whole_block(tokens, width),
        ],
        out_specs=whole_block(tokens, triple),
        out_shape=jax.ShapeDtypeStruct((windows, tokens, triple), jnp.bfloat16),
        cost_estimate=pl.CostEstimate(
            flops=8 * windows * tokens * tokens * width * 20, bytes_accessed=10000000, transcendentals=0
        ),
        name="attention_back",
    )(qkv_all, probs, d_context)


def target_table():
    edges = jnp.arange(BINS + 1, dtype=jnp.int32).astype(jnp.float32)
    centre = jnp.arange(BINS, dtype=jnp.int32).astype(jnp.float32)[:, None] + 0.5
    cumulative = 0.5 * jax.scipy.special.erf((edges - centre) / (smear * math.sqrt(2.0)))
    table = (cumulative[:, 1:] - cumulative[:, :-1]) / (cumulative[:, -1:] - cumulative[:, :1])
    upper = lax.reduce_precision(table, 8, 7)
    lower = (table - upper).astype(jnp.bfloat16)
    return (upper.astype(jnp.bfloat16), lower)


def head_grad(normed3, w_head, target_bins, land_mask):
    upper, lower = target_table()
    weight_tok = land_mask.astype(jnp.float32) / VARS
    bins = jnp.arange(BINS, dtype=jnp.int32)[None, :]
    pieces = []
    for var in range(VARS):
        logits = jnp.dot(
            normed3,
            w_head[:, var * BINS : (var + 1) * BINS],
            preferred_element_type=jnp.float32,
        )
        exponent = jnp.exp(logits - jnp.max(logits, -1, keepdims=True))
        bin_probs = exponent / jnp.sum(exponent, -1, keepdims=True)
        picked = (target_bins[:, var : var + 1] == bins).astype(jnp.bfloat16)
        target = jnp.dot(picked, upper, preferred_element_type=jnp.float32) + jnp.dot(
            picked, lower, preferred_element_type=jnp.float32
        )
        pieces.append((weight_tok * (bin_probs - target)).astype(jnp.bfloat16))
    return jnp.concatenate(pieces, 1)


def roll_ahead(block):
    half_rows = WIN_LAT // 2
    half_cols = WIN_LON // 2
    edge_cols = shifted_2(block[:, :half_cols], "lon", -1)
    moved_cols = jnp.concatenate([block[:, half_cols:], edge_cols], 1)
    edge_rows = shifted_2(moved_cols[:half_rows], "lat", -1)
    return jnp.concatenate([moved_cols[half_rows:], edge_rows], 0)


def roll_behind(block):
    half_rows = WIN_LAT // 2
    half_cols = WIN_LON // 2
    row_count, col_count = (block.shape[0], block.shape[1])
    edge_cols = shifted_2(block[:, col_count - half_cols :], "lon", 1)
    moved_cols = jnp.concatenate([edge_cols, block[:, : col_count - half_cols]], 1)
    edge_rows = shifted_2(moved_cols[row_count - half_rows :], "lat", 1)
    return jnp.concatenate([edge_rows, moved_cols[: row_count - half_rows]], 0)


def scatter_over(value, axis):
    return lax.psum_scatter(value, axis, scatter_dimension=0, tiled=True)


def local(latent, w_qkv, w_proj, w_fc1, w_fc2, w_head, target_bins, land_mask):
    row_count, col_count, feat_width = latent.shape
    half_rows = WIN_LAT // 2
    tokens = WIN_LAT * WIN_LON
    lat_total = row_count * lax.axis_size("lat")
    devices = lax.axis_size("lat") * lax.axis_size("lon")
    row_place = (
        lax.axis_index("lat") * row_count + jnp.arange(row_count, dtype=jnp.int32) + half_rows
    )
    row_labels = (row_place >= lat_total).astype(jnp.int32)
    window_tags = jnp.repeat(row_labels.reshape(-1, WIN_LAT), WIN_LON, axis=1)
    allowed = (window_tags[:, :, None] == window_tags[:, None, :]).astype(jnp.float32)
    marks = jnp.concatenate([target_bins, land_mask[:, :, None]], 2)
    residual_in = to_windows(roll_ahead(latent)).astype(jnp.float32)
    marks = to_windows(roll_ahead(marks))
    scaled1, inverse1 = normalize(residual_in)
    shifted = scaled1.astype(jnp.bfloat16)
    qkv_all = jnp.dot(shifted, w_qkv, preferred_element_type=jnp.float32).astype(jnp.bfloat16)
    qkv_all = qkv_all.reshape(-1, tokens, 3 * feat_width)
    context, attn_probs = attention(qkv_all, allowed, col_count // WIN_LON)
    context = context.reshape(-1, feat_width)
    attended = jnp.dot(context, w_proj, preferred_element_type=jnp.float32).astype(jnp.bfloat16)
    residual = residual_in + attended.astype(jnp.float32)
    scaled2, inverse2 = normalize(residual)
    normed2 = scaled2.astype(jnp.bfloat16)
    pre_act = jnp.dot(normed2, w_fc1, preferred_element_type=jnp.float32)
    activated, gelu_slope = gelu_parts(pre_act)
    activated = activated.astype(jnp.bfloat16)
    block_out = residual + jnp.dot(activated, w_fc2, preferred_element_type=jnp.float32)
    scaled3, inverse3 = normalize(block_out)
    normed3 = scaled3.astype(jnp.bfloat16)
    d_logits = head_grad(normed3, w_head, marks[:, :VARS], marks[:, VARS:])
    grad_head = jnp.dot(normed3.T, d_logits, preferred_element_type=jnp.float32)
    d_out = norm_back(
        scaled3, inverse3, jnp.dot(d_logits, w_head.T, preferred_element_type=jnp.float32)
    )
    d_outb = d_out.astype(jnp.bfloat16)
    grad_fc2 = jnp.dot(activated.T, d_outb, preferred_element_type=jnp.float32)
    d_pre = (jnp.dot(d_outb, w_fc2.T, preferred_element_type=jnp.float32) * gelu_slope).astype(
        jnp.bfloat16
    )
    grad_fc1 = jnp.dot(normed2.T, d_pre, preferred_element_type=jnp.float32)
    d_resid = d_out + norm_back(
        scaled2, inverse2, jnp.dot(d_pre, w_fc1.T, preferred_element_type=jnp.float32)
    )
    d_attended = d_resid.astype(jnp.bfloat16)
    grad_proj = jnp.dot(context.T, d_attended, preferred_element_type=jnp.float32)
    grads = [grad.astype(jnp.bfloat16) for grad in (grad_head, grad_fc1, grad_proj)]
    ratio = grad_fc2.shape[0] // feat_width
    low_fc2 = grad_fc2.astype(jnp.bfloat16).reshape(
        devices, ratio, feat_width // devices, feat_width
    )
    grads += [low_fc2[:, part].reshape(feat_width, feat_width) for part in range(ratio)]
    joined, d_attended = lax.optimization_barrier((jnp.concatenate(grads, 1), d_attended))
    early = scatter_over(joined, "lat")
    d_context = jnp.dot(d_attended, w_proj.T, preferred_element_type=jnp.float32).astype(
        jnp.bfloat16
    )
    d_qkv = attention_back(
        qkv_all, attn_probs, d_context.reshape(-1, tokens, feat_width)
    ).reshape(-1, 3 * feat_width)
    grad_qkv = jnp.dot(shifted.T, d_qkv, preferred_element_type=jnp.float32)
    late = scatter_over(grad_qkv.astype(jnp.bfloat16), "lat")
    summed = scatter_over(jnp.concatenate([late, early], 1), "lon").astype(jnp.float32)
    late, early = summed[:, : 3 * feat_width], summed[:, 3 * feat_width :]
    d_shifted = jnp.dot(d_qkv, w_qkv.T, preferred_element_type=jnp.float32).astype(jnp.bfloat16)
    grad_latent = (d_resid + norm_back(scaled1, inverse1, d_shifted.astype(jnp.float32))).astype(
        jnp.bfloat16
    )
    grad_latent = roll_behind(from_windows(grad_latent, row_count, col_count))
    cuts = [grad_head.shape[1], grad_fc1.shape[1], grad_proj.shape[1]]
    first, second, third = cuts[0], cuts[0] + cuts[1], sum(cuts)
    sum_fc2 = early[:, third:].reshape(-1, ratio, feat_width).transpose(1, 0, 2)
    return (
        grad_latent,
        late,
        early[:, second:third],
        early[:, first:second],
        sum_fc2.reshape(-1, feat_width),
        early[:, :first],
    )


def solution(mesh):
    placed = (
        P("lat", "lon", None),
        P(),
        P(),
        P(),
        P(),
        P(),
        P("lat", "lon", None),
        P("lat", "lon"),
    )
    return jax.shard_map(
        local,
        mesh=mesh,
        in_specs=placed,
        out_specs=(
            P("lat", "lon", None),
            P(("lat", "lon"), None),
            P(("lat", "lon"), None),
            P(("lat", "lon"), None),
            P(("lat", "lon"), None),
            P(("lat", "lon"), None),
        ),
        check_vma=False,
    )
```

time: 578 us -> 362 us (0.63); the launches traced: 569 us -> 361 us
  waiting for transfers between devices: 302 us -> 172 us
  local copies, waits for them, and re-layouts: 103 us -> 33.3 us
  Pallas kernels: 0 us -> 48.4 us
  matrix products: 97.6 us -> 59.3 us
  other arithmetic: 38.4 us -> 20.1 us
    reduce_scatter x10 -> x3, waiting for transfers between devices: 281 us -> 155 us  [scatter_over(): return lax.psum_scatter(value, axis, scatter_dimension=0, tiled=True)]
    pallas_call x0 -> x2, Pallas kernels: none -> 48.4 us  [the longest x1 34.3 us: attention_back(): pl.pallas_call(attention_back_kernel, grid=(windows,), in_specs=[whole_bl...]
    another operation x9 -> x0, local copies, waits for them, and re-layouts: 38.8 us -> none  [the longest x1 8.69 us: window_backward(): joined = jnp.stack([d_query, d_key, d_value], 2).astype(jnp.bfloat16)]
    dot_general x8 -> x14, matrix products: 37 us -> 21 us  [the longest x4 5.12 us: head_grad(): jnp.dot(picked, upper, preferred_element_type=jnp.float32)]
    unnamed x83 -> x47, local copies, waits for them, and re-layouts: 18.9 us -> 5.68 us
    sub x1 -> x0, matrix products: 12 us -> none  [head_grad(): exponent = jnp.exp(logits - highest)]
    convert_element_type x4 -> x5, local copies, waits for them, and re-layouts: 18.5 us -> 11.3 us  [the longest x3 8.76 us: local(): residual_in = to_windows(roll_ahead(latent)).astype(jnp.float32)]
    dot_general x2 -> x0, local copies, waits for them, and re-layouts: 6.48 us -> none  [the longest x1 4.18 us: local(): jnp.dot(d_logits, w_head.T, preferred_element_type=jnp.float32)]
  transfers between devices with their start and end apart: 18 -> 9, of which waited for: 14 -> 7; matrix products, arithmetic and copies ran while one was open for 19% -> 6% of each run, Pallas kernels for 0% -> 0%
where the time goes in v1:
time: 362 us; the launch traced here: 361 us
  waiting for transfers between devices  172 us (48%)
  matrix products  59.3 us (16%)
  Pallas kernels  48.4 us (13%)
  local copies, waits for them, and re-layouts  33.3 us (9%)
  other arithmetic  20.1 us (6%)
  between operations  14.3 us (4%)
  starting transfers between devices  13.6 us (4%)
    reduce_scatter x3, waiting for transfers between devices, scatter_over(): return lax.psum_scatter(value, axis, scatter_dimension=0, tiled=True)  155 us
    pallas_call x1, Pallas kernels, attention_back(): pl.pallas_call(attention_back_kernel, grid=(windows,), in_specs=[whole_bl...  34.3 us
    ppermute x6, waiting for transfers between devices, shifted_2(): return lax.ppermute(value, axis, pairs)  15.9 us
    pallas_call x1, Pallas kernels, attention(): pl.pallas_call(attention_kernel, grid=(windows,), in_specs=[whole_block(t...  14.1 us
    ppermute x6, starting transfers between devices, shifted_2(): return lax.ppermute(value, axis, pairs)  13.4 us
    convert_element_type x3, local copies, waits for them, and re-layouts, local(): residual_in = to_windows(roll_ahead(latent)).astype(jnp.float32)  8.76 us
  transfers between devices with their start and end apart: 9, of which 7 were waited for; matrix products, arithmetic and copies ran while one was open for 6% of the time, Pallas kernels for 0%

profile of v1, /device:TPU:0, one launch (start us, length us, event | category | flops | bytes accessed | tf_op | source)
XLA Modules:
  0.0 360.5 jit_solution(6954859639485760151)
XLA Ops:
  7.2 0.8 copy.40
  8.8 3.4 collective-permute-start.2
  12.2 1.5 slice.169
  16.2 0.8 slice_add_fusion
  17.4 3.6 collective-permute-start.3
  21.0 1.3 collective-permute-done.3
  23.2 1.1 reshape.169
  24.4 1.2 fusion.31
  25.6 1.3 fusion.32
  26.9 1.3 fusion.33
  28.3 1.2 fusion.34
  29.5 4.1 %collective-permute-start.1 = (bf16[3,72,512]{2,1,0:T(8,128)(2,1)S(1)}, bf16[3,72,512]{2,1,0:T(8,128)(2,1)S(1)}, u32[]{:S(2)}, u32[]{:S(2)}) collective-permute-start(bf16[3,72,512]{2,1,0:T(8,128)(2,1)S(1)} %pad_maximum_fusion.6), channel_id=1, source_target_pairs={{0,24},{8,0},{16,8},{24,16},{1,25},{9,1},{17,9},{25,17},{2,26},{10... | collective-permute-start | bytes 663560 | tf_op jit(solution)/shard_map/ppermute | solution.py:26
  33.8 3.4 collective-permute-done.1
  37.2 1.3 maximum_convert_fusion
  38.5 2.7 reshape.179
  41.2 2.0 bitcast_reduce_fusion
  44.7 3.4 copy.37
  48.2 2.6 reshape.177
  50.8 5.1 %convolution_convert_fusion = bf16[864,1536]{1,0:T(8,128)(2,1)} fusion(bf16[512,1536]{1,0:T(8,128)(2,1)} %param.9, f32[864,512]{1,0:T(8,128)} %reshape.177, f32[864]{0:T(1024)S(1)} %rsqrt.29, f32[864]{0:T(1024)S(1)} %div.161), kind=kOutput, calls=%fused_computation.9 | convolution fusion | flops 1361608704 | bytes 6003456 | tf_op jit(solution)/shard_map/dot_general | solution.py:234
  55.9 14.1 %attention.1 = (bf16[12,72,512]{2,1,0:T(8,128)(2,1)}, f32[12,8,72,72]{3,2,1,0:T(8,128)}) custom-call(bf16[12,72,1536]{2,1,0:T(8,128)(2,1)} %bitcast.81, f32[2,72,72]{2,1,0:T(8,128)} %compare_convert_fusion.allowed_ref), custom_call_target="tpu_custom_call" | custom-call | flops 2548039680 | bytes 8000000 | tf_op jit(solution)/shard_map/attention/pallas_call | solution.py:124
  69.9 2.6 fusion.76
  73.0 5.0 %multiply_convert_fusion = (bf16[864,2048]{1,0:T(8,128)(2,1)S(1)}, f32[864,2048]{1,0:T(8,128)}) fusion(bf16[512,2048]{1,0:T(8,128)(2,1)S(1)} %copy-done, f32[864,512]{1,0:T(8,128)S(1)} %get-tuple-element.35, f32[864]{0:T(1024)S(1)} %add_rsqrt_fusion.2, f32[864]{0:T(1024)S(1)} %broadcast_multiply_fusion.8), kind=kOutput, calls=%fused_computation.7 | convolution fusion | flops 1822113792 | bytes 14490368 | tf_op jit(solution)/shard_map/dot_general | solution.py:242
  78.1 2.1 fusion.77
  80.9 1.1 copy-done.8
  84.6 1.0 fusion.28
  85.8 1.0 fusion.27
  87.1 1.0 fusion.26
  88.5 1.2 fusion.25
  89.7 2.4 fusion.72
  92.1 2.3 fusion.12
  94.3 1.2 copy.49
  95.5 1.4 convert_element_type.205
  96.9 2.7 subtract_multiply_fusion
  99.6 4.6 %convolution_convert_fusion.2 = bf16[2048,512]{1,0:T(8,128)(2,1)S(1)} fusion(bf16[864,2048]{1,0:T(8,128)(2,1)} %copy-done.19, f32[864,512]{1,0:T(8,128)S(1)} %subtract_multiply_fusion), kind=kOutput, calls=%fused_computation.11 | convolution fusion | flops 1813430272 | bytes 7405568 | tf_op jit(solution)/shard_map/dot_general | solution.py:254
  104.2 4.3 %fusion.5 = bf16[864,2048]{1,0:T(8,128)(2,1)S(1)} fusion(f32[864,2048]{1,0:T(8,128)S(1)} %bitcast.87, bf16[2048,512]{1,0:T(8,128)(2,1)S(1)} %copy-done.18, f32[864,512]{1,0:T(8,128)S(1)} %subtract_multiply_fusion), kind=kOutput, calls=%fused_computation.6 | convolution fusion | flops 1830076416 | bytes 14483456 | tf_op jit(solution)/shard_map/dot_general | solution.py:255
  108.7 1.3 copy-done.3
  110.0 2.2 fusion.71
  112.2 4.0 %fusion.6 = bf16[512,5632]{1,0:T(8,128)(2,1)} fusion(bf16[512,5632]{1,0:T(8,128)(2,1)} %fusion.12, bf16[864,2048]{1,0:T(8,128)(2,1)S(1)} %fusion.5, f32[864,512]{1,0:T(8,128)S(1)} %copy-done.3, f32[864]{0:T(1024)S(1)} %add_rsqrt_fusion.2, f32[864]{0:T(1024)S(1)} %broadcast_multiply_fusion.8), kind=kOutput, calls=%fused_computation.13 | convolution fusion | flops 1814315008 | bytes 7412480 | tf_op jit(solution)/shard_map/dot_general | solution.py:258
  116.1 1.8 fusion.73
  117.9 1.6 fusion.24
  119.5 0.9 constant_dynamic-update-slice_fusion.3
  120.5 0.9 constant_dynamic-update-slice_fusion.2
  121.4 0.9 constant_dynamic-update-slice_fusion.1
  122.3 0.9 constant_dynamic-update-slice_fusion
  123.1 2.7 convolution_convert_fusion.6
  125.9 34.3 %attention_back.1 = bf16[12,72,1536]{2,1,0:T(8,128)(2,1)} custom-call(bf16[12,72,1536]{2,1,0:T(8,128)(2,1)} %bitcast.82, f32[12,8,72,72]{3,2,1,0:T(8,128)} %get-tuple-element.11.probs_ref, bf16[12,72,512]{2,1,0:T(8,128)(2,1)} %bitcast.85), custom_call_target="tpu_custom_call" | custom-call | flops 5096079360 | bytes 10000000 | tf_op jit(solution)/shard_map/attention_back/pallas_call | solution.py:146
  160.2 4.7 %convolution_convert_fusion.1 = bf16[512,1536]{1,0:T(8,128)(2,1)} fusion(bf16[864,512]{1,0:T(8,128)(2,1)S(1)} %convert_element_type.205, bf16[864,1536]{1,0:T(8,128)(2,1)} %bitcast.83), kind=kOutput, calls=%fused_computation.10 | convolution fusion | flops 1359740928 | bytes 5111808 | tf_op jit(solution)/shard_map/dot_general | solution.py:278
  165.7 34.8 %reduce-scatter.4.cloned.1.call-done = bf16[128,1536]{1,0:T(8,128)(2,1)} async-done(((bf16[512,1536]{1,0:T(8,128)(2,1)}), bf16[128,1536]{1,0:T(8,128)(2,1)}) %reduce-scatter.4.cloned.1.call-update) | async-done | bytes 393232 | tf_op jit(solution)/shard_map/reduce_scatter | solution.py:214
  200.6 103.5 %reduce-scatter.6.cloned.1.call-done = bf16[128,5632]{1,0:T(8,128)(2,1)} async-done(((bf16[512,5632]{1,0:T(8,128)(2,1)}), bf16[128,5632]{1,0:T(8,128)(2,1)}) %reduce-scatter.6.cloned.1.call-update) | async-done | bytes 1441808 | tf_op jit(solution)/shard_map/reduce_scatter | solution.py:214
  304.0 2.8 pad_maximum_fusion
  306.9 4.6 %convert_reduce_fusion = (f32[864]{0:T(1024)S(1)}, f32[864]{0:T(1024)S(1)}, bf16[864,512]{1,0:T(8,128)(2,1)S(1)}) fusion(f32[864]{0:T(1024)S(1)} %rsqrt.29, f32[864,512]{1,0:T(8,128)} %reshape.177, f32[864]{0:T(1024)S(1)} %div.161, bf16[864,1536]{1,0:T(8,128)(2,1)} %bitcast.84, bf16[512,1536]{1,0:T(8,128)(2,1)} %param.9), kind=kOutput, calls=%fused_computation.16 | convolution fusion | flops 1362049280 | bytes 6895104 | tf_op jit(solution)/shard_map/dot_general | solution.py:282
  311.5 1.6 fusion.10
  313.1 1.3 reshape.173
  314.4 1.1 copy.48
  315.5 1.4 reshape.174
  317.0 4.9 %collective-permute-done.4 = bf16[12,6,512]{2,1,0:T(8,128)(2,1)S(1)} collective-permute-done((bf16[12,6,512]{2,1,0:T(8,128)(2,1)S(1)}, bf16[12,6,512]{2,1,0:T(8,128)(2,1)S(1)}, u32[]{:S(2)}, u32[]{:S(2)}) %collective-permute-start.4) | collective-permute-done | bytes 73760 | tf_op jit(solution)/shard_map/ppermute | solution.py:26
  322.0 1.6 collective-permute-start.5
  323.6 6.2 %collective-permute-done.5 = bf16[3,72,512]{2,1,0:T(8,128)(2,1)S(1)} collective-permute-done((bf16[3,72,512]{2,1,0:T(8,128)(2,1)S(1)}, bf16[3,72,512]{2,1,0:T(8,128)(2,1)S(1)}, u32[]{:S(2)}, u32[]{:S(2)}) %collective-permute-start.5) | collective-permute-done | bytes 221216 | tf_op jit(solution)/shard_map/ppermute | solution.py:26
  329.8 1.1 fusion.30
  330.9 16.6 %reduce-scatter.8.cloned.1.call-done = bf16[16,7168]{1,0:T(8,128)(2,1)} async-done(((bf16[128,7168]{1,0:T(8,128)(2,1)}), bf16[16,7168]{1,0:T(8,128)(2,1)}) %reduce-scatter.8.cloned.1.call-update) | async-done | bytes 229392 | tf_op jit(solution)/shard_map/reduce_scatter | solution.py:214
  347.5 1.5 fusion.75
  349.8 1.3 slice.224
  351.2 1.4 slice.227
  352.6 1.4 slice.223
  (107 shorter events, 12.5 us)
Async XLA Ops:
  7.2 65.8 %copy-start = (bf16[512,2048]{1,0:T(8,128)(2,1)S(1)}, bf16[512,2048]{1,0:T(8,128)(2,1)}, u32[]{:S(2)}) copy-start(bf16[512,2048]{1,0:T(8,128)(2,1)} %param.11) | copy-start | bytes 6291460
  7.2 193.4 %reduce-scatter.4.cloned.1.call-start = ((), (), s32[]{:S(2)}) async-start(), calls=%async_computation.3 | async-start | bytes 1966080 | tf_op jit(solution)/shard_map/reduce_scatter | solution.py:214
  8.8 8.4 %collective-permute-start.2 = (s32[12,6,5]{1,2,0:T(8,128)S(1)}, s32[12,6,5]{1,2,0:T(8,128)S(1)}, u32[]{:S(2)}, u32[]{:S(2)}) collective-permute-start(s32[12,6,5]{1,2,0:T(8,128)S(1)} %pad_add_fusion), channel_id=1, source_target_pairs={{0,7},{1,0},{2,1},{3,2},{4,3},{5,4},{6,5},{7,6},{8,15},{9,8},{10,9... | collective-permute-start | bytes 4328 | tf_op jit(solution)/shard_map/ppermute | solution.py:26
  13.8 15.7 %collective-permute-start = (bf16[12,6,512]{2,1,0:T(8,128)(2,1)}, bf16[12,6,512]{2,1,0:T(8,128)(2,1)S(1)}, u32[]{:S(2)}, u32[]{:S(2)}) collective-permute-start(bf16[12,6,512]{2,1,0:T(8,128)(2,1)} %slice.169), channel_id=1, source_target_pairs={{0,7},{1,0},{2,1},{3,2},{4,3},{5,4},{6,5},{7,6},{8,15},{9,8},{10,9... | collective-permute-start | bytes 221192 | tf_op jit(solution)/shard_map/ppermute | solution.py:26
  14.6 2.4 copy-start.7
  17.4 5.0 %collective-permute-start.3 = (s32[3,72,5]{1,2,0:T(8,128)S(1)}, s32[3,72,5]{1,2,0:T(8,128)S(1)}, u32[]{:S(2)}, u32[]{:S(2)}) collective-permute-start(s32[3,72,5]{1,2,0:T(8,128)S(1)} %pad_add_fusion.2), channel_id=1, source_target_pairs={{0,24},{8,0},{16,8},{24,16},{1,25},{9,1},{17,9},{25,17},{2,26},{10... | collective-permute-start | bytes 12968 | tf_op jit(solution)/shard_map/ppermute | solution.py:26
  29.5 7.7 %collective-permute-start.1 = (bf16[3,72,512]{2,1,0:T(8,128)(2,1)S(1)}, bf16[3,72,512]{2,1,0:T(8,128)(2,1)S(1)}, u32[]{:S(2)}, u32[]{:S(2)}) collective-permute-start(bf16[3,72,512]{2,1,0:T(8,128)(2,1)S(1)} %pad_maximum_fusion.6), channel_id=1, source_target_pairs={{0,24},{8,0},{16,8},{24,16},{1,25},{9,1},{17,9},{25,17},{2,26},{10... | collective-permute-start | bytes 663560 | tf_op jit(solution)/shard_map/ppermute | solution.py:26
  41.2 2.4 copy-start.1
  72.6 5.5 %copy-start.2 = (f32[864,512]{1,0:T(8,128)}, f32[864,512]{1,0:T(8,128)S(1)}, u32[]{:S(2)}) copy-start(f32[864,512]{1,0:T(8,128)S(1)} %get-tuple-element.35) | copy-start | bytes 5308420
  73.0 5.0 %copy-start.17 = (bf16[2048,512]{1,0:T(8,128)(2,1)S(1)}, bf16[2048,512]{1,0:T(8,128)(2,1)}, u32[]{:S(2)}) copy-start(bf16[2048,512]{1,0:T(8,128)(2,1)} %param.12) | copy-start | bytes 6291460
  78.1 2.1 copy-start.19
  80.1 9.6 %copy-start.5 = (f32[864,512]{1,0:T(8,128)}, f32[864,512]{1,0:T(8,128)S(1)}, u32[]{:S(2)}) copy-start(f32[864,512]{1,0:T(8,128)S(1)} %get-tuple-element.39) | copy-start | bytes 5308420
  80.6 1.4 copy-start.8
  83.4 1.2 copy-start.12
  83.4 1.2 copy-start.16
  84.6 1.2 copy-start.11
  85.8 1.3 copy-start.10
  87.1 1.4 copy-start.9
  96.9 7.3 %slice-start = ((s8[7077888]{0:T(1024)(128)(4,1)}), s8[4194304]{0:T(1024)(128)(4,1)S(1)}, s32[]{:S(2)}) async-start(s8[7077888]{0:T(1024)(128)(4,1)} %bitcast.86), calls=%async_computation.6 | async-start | bytes 8388608
  99.6 4.6 %copy-start.18 = (bf16[2048,512]{1,0:T(8,128)(2,1)S(1)}, bf16[2048,512]{1,0:T(8,128)(2,1)}, u32[]{:S(2)}) copy-start(bf16[2048,512]{1,0:T(8,128)(2,1)} %param.12) | copy-start | bytes 6291460
  99.6 4.6 %slice-start.1 = ((s8[7077888]{0:T(1024)(128)(4,1)}), s8[2883584]{0:T(1024)(128)(4,1)S(1)}, s32[]{:S(2)}) async-start(s8[7077888]{0:T(1024)(128)(4,1)} %bitcast.86), calls=%async_computation.7 | async-start | bytes 5767168
  108.5 1.5 copy-start.3
  116.1 1.8 copy-start.13
  117.9 2.6 copy-start.14
  120.5 2.7 copy-start.15
  164.9 139.1 %reduce-scatter.6.cloned.1.call-start = ((), (), s32[]{:S(2)}) async-start(), calls=%async_computation.4 | async-start | bytes 7208960 | tf_op jit(solution)/shard_map/reduce_scatter | solution.py:214
  165.7 181.8 %reduce-scatter.8.cloned.1.call-start = ((), (), s32[]{:S(2)}) async-start(), calls=%async_computation.5 | async-start | bytes 2064384 | tf_op jit(solution)/shard_map/reduce_scatter | solution.py:214
  306.9 4.6 %copy-start.4 = (f32[864,512]{1,0:T(8,128)S(1)}, f32[864,512]{1,0:T(8,128)}, u32[]{:S(2)}) copy-start(f32[864,512]{1,0:T(8,128)} %reshape.177) | copy-start | bytes 5308420
  306.9 4.6 %copy-start.6 = (f32[864,512]{1,0:T(8,128)S(1)}, f32[864,512]{1,0:T(8,128)}, u32[]{:S(2)}) copy-start(f32[864,512]{1,0:T(8,128)} %get-tuple-element.25) | copy-start | bytes 5308420
  317.0 5.0 %collective-permute-start.4 = (bf16[12,6,512]{2,1,0:T(8,128)(2,1)S(1)}, bf16[12,6,512]{2,1,0:T(8,128)(2,1)S(1)}, u32[]{:S(2)}, u32[]{:S(2)}) collective-permute-start(bf16[12,6,512]{2,1,0:T(8,128)(2,1)S(1)} %slice.221), channel_id=1, source_target_pairs={{0,1},{1,2},{2,3},{3,4},{4,5},{5,6},{6,7},{7,0},{8,9},{9,10},{10,1... | collective-permute-start | bytes 221192 | tf_op jit(solution)/shard_map/ppermute | solution.py:26
  322.0 7.8 %collective-permute-start.5 = (bf16[3,72,512]{2,1,0:T(8,128)(2,1)S(1)}, bf16[3,72,512]{2,1,0:T(8,128)(2,1)S(1)}, u32[]{:S(2)}, u32[]{:S(2)}) collective-permute-start(bf16[3,72,512]{2,1,0:T(8,128)(2,1)S(1)} %pad_maximum_fusion.5), channel_id=1, source_target_pairs={{0,8},{8,16},{16,24},{24,0},{1,9},{9,17},{17,25},{25,1},{2,10},{10... | collective-permute-start | bytes 663560 | tf_op jit(solution)/shard_map/ppermute | solution.py:26
Sparse Core Ops, SparseCore 0:
  165.0 35.4 reduce-scatter.3
  202.9 101.1 reduce-scatter.5
  307.4 40.0 reduce-scatter.7
